TPU v7x, 32 devices: a whole 2x2x4 slice. The times are simulated.
32 devices in a mesh: row: 2 (over y), theta: 4 (over x, core), gz: 4 (over z).
Axes of the slice: x: 2, y: 2, z: 4, core: 2. Of those that a mesh axis runs over, the one named last changes fastest.
Arguments:
- state_start: float32 [6, 8, 128, 1024], P(None, 'row', 'gz', 'theta'), may hold values from -1.2 to 1.2
- state_section: float32 [6, 8, 128, 1024], P(None, 'row', 'gz', 'theta'), may hold values from -1.5 to 4, as said below
- phase: int32 [8, 128, 1024], P('row', 'gz', 'theta'), may hold values 0 or 1
- cutoff: int32 [4], replicated, may hold values from 1 to 63
Outputs:
- state_next: float32 [6, 8, 128, 1024], P(None, 'row', 'gz', 'theta')
Inputs may be any that keep to these rules, and one draw needn't show every extreme that they name: `state_section`: channel 0 (density) lies in 0.5 to 2.0, channels 1 to 3 (momenta) in -1.5 to 1.5, channel 4 (total energy) in 2.5 to 4.0, channel 5 (jet mass density) in 0 to 1.0.
All inputs are finite; a program needn't handle non-finite values. No bound on the sum of `phase` on one device may be relied on, other than what follows from the above.
Results may differ from a plain program's by a relative error of at most 0.0003.
Values sent between devices are 32-bit elements; how exact they have to be, the bound alone decides.
A program may use at most 64 MiB of HBM per device.

v0:
```python
import math
import jax
import jax.numpy as jnp
from jax import lax
from jax.sharding import PartitionSpec as P

NT = 1024
KMODES = 64
split_speed = 10.0
time_step = 0.05
weno_epsilon = 1e-06
liquid_ratio = 4.4
gas_ratio = 1.4
liquid_stiffness = 0.6


def passed_along(value, axis, steps):
    count = lax.axis_size(axis)
    pairs = [(source, (source + steps) % count) for source in range(count)]
    return lax.ppermute(value, axis, pairs)


def with_halo(cells, sides, width):
    for axis, dim in sides:
        count = lax.axis_size(axis)
        head = lax.slice_in_dim(cells, 0, width, axis=dim)
        tail = lax.slice_in_dim(cells, cells.shape[dim] - width, cells.shape[dim], axis=dim)
        cells = jnp.concatenate(
            [
                lax.ppermute(tail, axis, [(i, (i + 1) % count) for i in range(count)]),
                cells,
                lax.ppermute(head, axis, [((i + 1) % count, i) for i in range(count)]),
            ],
            axis=dim,
        )
    return cells


def pressure_of(state, phase):
    density = state[0]
    kinetic = 0.5 * (state[1] * state[1] + state[2] * state[2] + state[3] * state[3]) / density
    liquid = phase == 1
    heat_ratio = jnp.where(liquid, liquid_ratio, gas_ratio)
    stiffness = jnp.where(liquid, liquid_stiffness, 0.0)
    return (heat_ratio - 1.0) * (state[4] - kinetic) - heat_ratio * stiffness


def weno_face(far_left, near_left, centre, near_right, far_right):
    smooth_left = (
        13.0 / 12.0 * (far_left - 2.0 * near_left + centre) ** 2
        + 0.25 * (far_left - 4.0 * near_left + 3.0 * centre) ** 2
    )
    smooth_mid = (
        13.0 / 12.0 * (near_left - 2.0 * centre + near_right) ** 2
        + 0.25 * (near_left - near_right) ** 2
    )
    smooth_right = (
        13.0 / 12.0 * (centre - 2.0 * near_right + far_right) ** 2
        + 0.25 * (3.0 * centre - 4.0 * near_right + far_right) ** 2
    )
    weight_left = 0.1 / (weno_epsilon + smooth_left) ** 2
    weight_mid = 0.6 / (weno_epsilon + smooth_mid) ** 2
    weight_right = 0.3 / (weno_epsilon + smooth_right) ** 2
    weight_sum = weight_left + weight_mid + weight_right
    value_left = (2.0 * far_left - 7.0 * near_left + 11.0 * centre) / 6.0
    value_mid = (-near_left + 5.0 * centre + 2.0 * near_right) / 6.0
    value_right = (2.0 * centre + 5.0 * near_right - far_right) / 6.0
    return (
        weight_left * value_left + weight_mid * value_mid + weight_right * value_right
    ) / weight_sum


def face_fluxes(padded_line, array_axis, component):
    density = padded_line[0]
    velocity = padded_line[component] / density
    pressure_field = padded_line[6]
    conserved = padded_line[:6]
    flux_rows = [conserved[channel] * velocity for channel in range(6)]
    flux_rows[component] = flux_rows[component] + pressure_field
    flux_rows[4] = flux_rows[4] + pressure_field * velocity
    physical = jnp.stack(flux_rows)
    upward = 0.5 * (physical + split_speed * conserved)
    downward = 0.5 * (physical - split_speed * conserved)
    face_count = padded_line.shape[array_axis] - 5

    def shifted(values, offset):
        return lax.slice_in_dim(values, offset, offset + face_count, axis=array_axis)

    upwind_part = weno_face(
        shifted(upward, 0),
        shifted(upward, 1),
        shifted(upward, 2),
        shifted(upward, 3),
        shifted(upward, 4),
    )
    downwind_part = weno_face(
        shifted(downward, 5),
        shifted(downward, 4),
        shifted(downward, 3),
        shifted(downward, 2),
        shifted(downward, 1),
    )
    return upwind_part + downwind_part


def tendency(centre_cells, radial_line, axial_line, azimuth_line, cycle_start):
    cycle_count = centre_cells.shape[1]
    radial_flux = face_fluxes(radial_line, 1, 1)
    axial_flux = face_fluxes(axial_line, 2, 3)
    azimuth_flux = face_fluxes(azimuth_line, 3, 2)
    cycle_index = (cycle_start + lax.iota(jnp.int32, cycle_count + 1)).astype(centre_cells.dtype)
    face_radius = cycle_index[None, :, None, None]
    cell_radius = face_radius[:, :-1] + 0.5
    weighted = face_radius * radial_flux
    div_radial = (weighted[:, 1:] - weighted[:, :-1]) / cell_radius
    div_axial = axial_flux[:, :, 1:] - axial_flux[:, :, :-1]
    angle_step = 2.0 * math.pi / NT
    div_azimuth = (azimuth_flux[..., 1:] - azimuth_flux[..., :-1]) / (cell_radius * angle_step)
    density = centre_cells[0]
    swirl_speed = centre_cells[2] / density
    radius = cell_radius[0]
    source_radial = (centre_cells[2] * swirl_speed + centre_cells[6]) / radius
    source_swirl = -centre_cells[1] * swirl_speed / radius
    zero_field = jnp.zeros_like(density)
    source = jnp.stack(
        [zero_field, source_radial, source_swirl, zero_field, zero_field, zero_field]
    )
    return source - div_radial - div_axial - div_azimuth


def across_axis(partner):
    sign_flip = jnp.array([1.0, -1.0, -1.0, 1.0, 1.0, 1.0, 1.0], partner.dtype)[:, None, None, None]
    return partner[:, ::-1] * sign_flip


def build_table(positions, mode_count, length):
    orders = lax.iota(jnp.int32, mode_count)
    phases = positions[:, None] * orders[None, :] % length
    angles = phases.astype(jnp.float32) * (2.0 * math.pi / length)
    return jnp.concatenate([jnp.cos(angles), jnp.sin(angles)], 1)


def cycle_weights(cutoff, mode_count, length):
    orders = lax.iota(jnp.int32, mode_count)
    mode_scale = jnp.where(orders == 0, 1.0 / length, 2.0 / length)
    kept_modes = orders[None, :] <= cutoff[:, None]
    weight_half = jnp.where(kept_modes, mode_scale[None, :], 0.0)
    return jnp.concatenate([weight_half, weight_half], 1)


def apply_filter(cycle_block, weights, theta_id):
    local_theta = cycle_block.shape[3]
    positions = theta_id * local_theta + lax.iota(jnp.int32, local_theta)
    fourier_table = build_table(positions, KMODES, NT)
    coefficients = jnp.einsum(
        "vizt,tk->vizk", cycle_block, fourier_table, precision=lax.Precision.HIGHEST
    )
    coefficients = lax.psum(coefficients, "theta")
    coefficients = coefficients * weights[None, :, None, :]
    return jnp.einsum("vizk,tk->vizt", coefficients, fourier_table, precision=lax.Precision.HIGHEST)


def shards(state_start, state_section, phase, cutoff):
    row_count = lax.axis_size("row")
    row_id = lax.axis_index("row")
    theta_count = lax.axis_size("theta")
    theta_id = lax.axis_index("theta")
    cycle_count = state_section.shape[1]
    filtered_count = cutoff.shape[0]
    pressure_field = pressure_of(state_section, phase)
    fields = jnp.concatenate([state_section, pressure_field[None]], 0)
    partner = passed_along(fields[:, 0:3], "theta", theta_count // 2)
    mirror = across_axis(partner)
    outer_rim = jnp.repeat(fields[:, -1:], 3, axis=1)
    padded = with_halo(fields, (("row", 1), ("theta", 3), ("gz", 2)), 3)
    radial_line = padded[:, :, 3:-3, 3:-3]
    axial_line = padded[:, 3:-3, :, 3:-3]
    azimuth_line = padded[:, 3:-3, 3:-3, :]
    lower_rim = jnp.where(row_id == 0, mirror, radial_line[:, :3])
    upper_rim = jnp.where(row_id == row_count - 1, outer_rim, radial_line[:, -3:])
    radial_line = jnp.concatenate([lower_rim, fields, upper_rim], 1)
    tendencies = tendency(fields, radial_line, axial_line, azimuth_line, row_id * cycle_count)
    advanced = 0.75 * state_start + 0.25 * (state_section + time_step * tendencies)
    weights = cycle_weights(cutoff, KMODES, NT)
    filtered = apply_filter(advanced, weights, theta_id)
    inner_next = jnp.where(row_id == 0, filtered, advanced)
    return jnp.concatenate([inner_next, advanced[:, filtered_count:]], 1)


def solution(mesh):
    in_specs = (
        P(None, "row", "gz", "theta"),
        P(None, "row", "gz", "theta"),
        P("row", "gz", "theta"),
        P(),
    )
    out_specs = P(None, "row", "gz", "theta")
    return jax.shard_map(shards, mesh=mesh, in_specs=in_specs, out_specs=out_specs, check_vma=False)
```

profile of v0, /device:TPU:0, one launch (start us, length us, event | category | flops | bytes accessed | tf_op | source)
XLA Modules:
  0.0 148.2 jit_solution(16903499594754744437)
XLA Ops:
  6.6 1.4 bitcast_dynamic-update-slice_fusion
  7.9 0.1 copy-done
  8.0 1.2 fusion.11
  9.2 3.0 %collective-permute-start.2 = (f32[7,3,32,256]{3,2,1,0:T(8,128)}, f32[7,3,32,256]{3,2,1,0:T(8,128)S(1)}, u32[]{:S(2)}, u32[]{:S(2)}) collective-permute-start(f32[7,3,32,256]{3,2,1,0:T(8,128)} %get-tuple-element.24), channel_id=1, source_target_pairs={{16,0},{0,16},{17,1},{1,17},{18,2},{2,18},{19,3},{3,19},{20,4},{4,... | collective-permute-start | bytes 2064392 | tf_op jit(solution)/shard_map/ppermute | solution.py:32
  12.2 1.5 %collective-permute-start = (f32[7,3,32,256]{3,2,1,0:T(8,128)}, f32[7,3,32,256]{3,2,1,0:T(8,128)}, u32[]{:S(2)}, u32[]{:S(2)}) collective-permute-start(f32[7,3,32,256]{3,2,1,0:T(8,128)} %get-tuple-element.24), channel_id=1, source_target_pairs={{0,8},{4,12},{8,0},{12,4},{1,9},{5,13},{9,1},{13,5},{2,10},{6,14},... | collective-permute-start | bytes 2064392 | tf_op jit(solution)/shard_map/ppermute | solution.py:20
  13.7 0.5 collective-permute-start.1
  14.2 0.1 divide_dynamic-update-slice_fusion
  14.4 0.0 copy-start.10
  14.4 0.0 copy-start.7
  14.5 0.6 fusion.47
  15.1 13.7 %collective-permute-done.2 = f32[7,3,32,256]{3,2,1,0:T(8,128)S(1)} collective-permute-done((f32[7,3,32,256]{3,2,1,0:T(8,128)}, f32[7,3,32,256]{3,2,1,0:T(8,128)S(1)}, u32[]{:S(2)}, u32[]{:S(2)}) %collective-permute-start.2) | collective-permute-done | bytes 688160 | tf_op jit(solution)/shard_map/ppermute | solution.py:32
  28.7 0.1 broadcast_select_fusion
  28.8 13.8 %collective-permute-done.1 = f32[7,3,32,256]{3,2,1,0:T(8,128)S(1)} collective-permute-done((f32[7,3,32,256]{3,2,1,0:T(8,128)}, f32[7,3,32,256]{3,2,1,0:T(8,128)S(1)}, u32[]{:S(2)}, u32[]{:S(2)}) %collective-permute-start.1) | collective-permute-done | bytes 688160 | tf_op jit(solution)/shard_map/ppermute | solution.py:30
  42.6 0.0 collective-permute-done
  42.6 1.5 %multiply_select_fusion = f32[7,3,32,256]{3,2,1,0:T(8,128)S(1)} fusion(f32[7,3,32,256]{3,2,1,0:T(8,128)S(1)} %collective-permute-done.1, f32[7,3,32,256]{3,2,1,0:T(8,128)} %collective-permute-done, f32[7]{0:T(128)S(1)} %copy-done.10, pred[]{:T(512)S(6)} %eq.25), kind=kLoop, calls=%fused_computation.37 | loop fusion | flops 344064 | bytes 2064413 | tf_op jit(solution)/shard_map/jit(_where)/select_n | solution.py:179
  44.2 1.9 %pad_maximum_fusion.2 = (f32[7,10,32,256]{3,2,1,0:T(8,128)}, f32[7,10,32,256]{3,2,1,0:T(8,128)S(1)}) fusion(f32[7,3,32,256]{3,2,1,0:T(8,128)S(1)} %broadcast_select_fusion, f32[1,4,32,256]{3,2,1,0:T(8,128)S(1)} %bitcast.49, f32[6,4,32,256]{3,2,1,0:T(8,128)S(1)} %copy-done, f32[7,3,32,256]{3,2,1,0:T(8,128)S(1)} %multiply_select_fusion, ...), kind=kLoop, calls=%fused_computation.2 | loop fusion | flops 2867200 | bytes 8257536 | tf_op jit(solution)/shard_map/concatenate | solution.py:181
  46.1 1.8 %fusion.56 = (f32[7,10,32,3]{3,2,1,0:T(8,128)}, f32[7,10,32,3]{3,2,1,0:T(8,128)}) fusion(f32[7,10,32,256]{3,2,1,0:T(8,128)S(1)} %get-tuple-element.22), kind=kLoop, calls=%fused_computation.127 | loop fusion | bytes 107520 | tf_op jit(solution)/shard_map/slice | solution.py:27
  47.9 2.6 %copy.7 = f32[7,10,32,3]{2,0,3,1:T(8,128)} copy(f32[7,10,32,3]{3,2,1,0:T(8,128)} %get-tuple-element.20) | data formatting | bytes 53760 | tf_op jit(solution)/shard_map/slice | solution.py:26
  50.5 0.3 collective-permute-start.4
  50.8 2.4 %copy.6 = f32[7,10,32,3]{2,0,3,1:T(8,128)} copy(f32[7,10,32,3]{3,2,1,0:T(8,128)} %get-tuple-element.19) | data formatting | bytes 53760 | tf_op jit(solution)/shard_map/slice | solution.py:27
  53.2 0.2 collective-permute-start.3
  53.4 0.1 multiply_dynamic-update-slice_fusion
  53.5 0.1 add_dynamic-update-slice_fusion
  53.7 0.1 fusion.16
  53.8 0.7 add_multiply_fusion
  54.5 5.2 %add_multiply_fusion.3 = f32[6,5,32,256]{3,2,1,0:T(8,128)} fusion(f32[6,10,32,256]{3,2,1,0:T(8,128)S(1)} %get-tuple-element.16, f32[6,10,32,256]{3,2,1,0:T(8,128)S(1)} %get-tuple-element.15, f32[5]{0:T(128)S(1)} %add_convert_fusion), kind=kLoop, calls=%fused_computation.20 | loop fusion | flops 31948800 | bytes 10813460 | tf_op jit(solution)/shard_map/mul | solution.py:114
  59.7 1.4 copy.9
  61.1 0.0 collective-permute-done.3
  61.1 1.4 copy.8
  62.5 2.6 %pad_maximum_fusion.1 = f32[7,10,32,262]{3,2,1,0:T(8,128)S(1)} fusion(f32[7,10,32,3]{3,2,1,0:T(8,128)S(1)} %copy.9, f32[7,3,32,256]{3,2,1,0:T(8,128)} %copy-done.3, f32[1,4,32,256]{3,2,1,0:T(8,128)S(1)} %bitcast.50, f32[6,4,32,256]{3,2,1,0:T(8,128)S(1)} %copy-done, f32[7,3,32,256]{3,2,1,0:T(8,128)} %copy-done.1, f32[7,10,32,3]{3,2,1,0:T(8,128)S(1)} %copy.8), kind=kLoop, calls=%fused_computation.1 | loop fusion | flops 2934400 | bytes 4695040 | tf_op jit(solution)/shard_map/concatenate | solution.py:28
  65.1 0.2 fusion.55
  65.2 0.9 copy-done.2
  66.1 0.2 copy-done.4
  66.4 0.2 multiply_dynamic-update-slice_fusion.1
  66.6 0.3 fusion.26
  66.8 0.3 fusion.25
  67.1 0.3 fusion.23
  67.4 0.3 fusion.22
  67.7 0.3 fusion.20
  68.0 0.3 add_multiply_fusion.1
  68.3 3.9 %collective-permute-start.6 = (f32[7,10,3,262]{3,2,1,0:T(4,128)S(1)}, f32[7,10,3,262]{3,2,1,0:T(4,128)S(1)}, u32[]{:S(2)}, u32[]{:S(2)}) collective-permute-start(f32[7,10,3,262]{3,2,1,0:T(4,128)S(1)} %get-tuple-element.18), channel_id=1, source_target_pairs={{1,0},{2,1},{3,2},{0,3},{5,4},{6,5},{7,6},{4,7},{9,8},{10,9},{11,1... | collective-permute-start | bytes 660248 | tf_op jit(solution)/shard_map/ppermute | solution.py:32
  72.2 0.0 collective-permute-start.5
  72.2 5.9 %divide_add_fusion = f32[6,4,32,257]{3,2,1,0:T(8,128)S(1)} fusion(f32[6,4,32,262]{3,2,1,0:T(8,128)S(1)} %get-tuple-element.14, f32[6,4,32,262]{3,2,1,0:T(8,128)S(1)} %get-tuple-element.13), kind=kLoop, calls=%fused_computation.13 | loop fusion | flops 25461504 | bytes 8684544 | tf_op jit(solution)/shard_map/add | solution.py:103
  78.1 4.3 %collective-permute-done.6 = f32[7,10,3,262]{3,2,1,0:T(4,128)S(1)} collective-permute-done((f32[7,10,3,262]{3,2,1,0:T(4,128)S(1)}, f32[7,10,3,262]{3,2,1,0:T(4,128)S(1)}, u32[]{:S(2)}, u32[]{:S(2)}) %collective-permute-start.6) | collective-permute-done | bytes 220112 | tf_op jit(solution)/shard_map/ppermute | solution.py:32
  82.4 10.1 %collective-permute-done.5 = f32[7,10,3,262]{3,2,1,0:T(4,128)S(1)} collective-permute-done((f32[7,10,3,262]{3,2,1,0:T(4,128)S(1)}, f32[7,10,3,262]{3,2,1,0:T(4,128)S(1)}, u32[]{:S(2)}, u32[]{:S(2)}) %collective-permute-start.5) | collective-permute-done | bytes 220112 | tf_op jit(solution)/shard_map/ppermute | solution.py:30
  92.5 5.7 %pad_maximum_fusion = f32[7,10,38,262]{3,2,1,0:T(8,128)S(1)} fusion(f32[7,10,3,262]{3,2,1,0:T(4,128)S(1)} %collective-permute-done.6, f32[7,10,32,3]{3,2,1,0:T(8,128)S(1)} %copy.9, f32[7,3,32,256]{3,2,1,0:T(8,128)S(1)} %copy-done.4, f32[1,4,32,256]{3,2,1,0:T(8,128)S(1)} %bitcast.57, f32[6,4,32,256]{3,2,1,0:T(8,128)S(1)} %copy-done, ...), kind=kLoop, calls=%fused_computation | loop fusion | flops 4878440 | bytes 5575360 | tf_op jit(solution)/shard_map/concatenate | solution.py:28
  98.2 0.2 multiply_dynamic-update-slice_fusion.2
  98.4 0.1 fusion.32
  98.5 0.1 fusion.31
  98.6 0.2 add_dynamic-update-slice_fusion.1
  98.8 0.2 fusion.30
  98.9 0.1 fusion.28
  99.1 0.3 add_multiply_fusion.2
  99.4 0.0 copy-start.8
  99.4 0.0 copy-start.9
  99.4 5.0 %divide_add_fusion.1 = f32[6,4,33,256]{3,2,1,0:T(8,128)S(1)} fusion(f32[6,4,38,256]{3,2,1,0:T(8,128)S(1)} %get-tuple-element.12, f32[6,4,38,256]{3,2,1,0:T(8,128)S(1)} %get-tuple-element.11), kind=kLoop, calls=%fused_computation.17 | loop fusion | flops 26155008 | bytes 8921088 | tf_op jit(solution)/shard_map/add | solution.py:103
  104.5 0.7 fusion.7
  105.2 0.0 copy-start.11
  105.2 1.6 %fusion.48 = f32[6,4,32,128]{3,2,1,0:T(8,128)} fusion(f32[6,4,32,256]{3,2,1,0:T(8,128)S(1)} %fusion.7, f32[256,64]{1,0:T(8,128)S(1)} %get-tuple-element.26, f32[256,64]{1,0:T(8,128)S(1)} %get-tuple-element.25), kind=kOutput, calls=%fused_computation.112 | convolution fusion | flops 302022656 | bytes 1310720 | tf_op jit(solution)/shard_map/vizt,tk->vizk/dot_general | solution.py:155
  106.8 0.0 all-reduce.2.cloned.1.call-update
  106.8 0.1 fusion.49
  106.9 0.1 pad_maximum_fusion.8
  107.0 31.6 %all-reduce.2.cloned.1.call-done = f32[6,4,32,128]{3,2,1,0:T(8,128)} async-done(((f32[6,4,32,128]{3,2,1,0:T(8,128)}), f32[6,4,32,128]{3,2,1,0:T(8,128)}) %all-reduce.2.cloned.1.call-update) | async-done | bytes 393232 | tf_op jit(solution)/shard_map/psum | solution.py:158
  138.6 2.7 %convolution_select_fusion = f32[6,4,32,256]{3,2,1,0:T(8,128)} fusion(f32[6,4,32,256]{3,2,1,0:T(8,128)S(1)} %fusion.7, f32[6,4,32,128]{3,2,1,0:T(8,128)} %all-reduce.2.cloned.1.call-done, pred[]{:T(512)S(6)} %eq.25, f32[4,128]{1,0:T(4,128)S(1)} %pad_maximum_fusion.8, f32[256,64]{1,0:T(8,128)S(1)} %get-tuple-element.26, f32[256,64]{1,0:T(8,128)S(1)} %get-tuple-element.25), kind=kOutput, calls=%fused_computation.9 | convolution fusion | flops 302317568 | bytes 2099201 | tf_op jit(solution)/shard_map/vizk,tk->vizt/dot_general | solution.py:160
  (30 shorter events, 0.3 us)
Async XLA Ops:
  6.5 1.5 copy-start
  6.5 132.1 %all-reduce.2.cloned.1.call-start = ((), (), s32[]{:S(2)}) async-start(), calls=%async_computation | async-start | bytes 786432 | tf_op jit(solution)/shard_map/psum | solution.py:158
  9.2 19.5 %collective-permute-start.2 = (f32[7,3,32,256]{3,2,1,0:T(8,128)}, f32[7,3,32,256]{3,2,1,0:T(8,128)S(1)}, u32[]{:S(2)}, u32[]{:S(2)}) collective-permute-start(f32[7,3,32,256]{3,2,1,0:T(8,128)} %get-tuple-element.24), channel_id=1, source_target_pairs={{16,0},{0,16},{17,1},{1,17},{18,2},{2,18},{19,3},{3,19},{20,4},{4,... | collective-permute-start | bytes 2064392 | tf_op jit(solution)/shard_map/ppermute | solution.py:32
  12.2 30.4 %collective-permute-start = (f32[7,3,32,256]{3,2,1,0:T(8,128)}, f32[7,3,32,256]{3,2,1,0:T(8,128)}, u32[]{:S(2)}, u32[]{:S(2)}) collective-permute-start(f32[7,3,32,256]{3,2,1,0:T(8,128)} %get-tuple-element.24), channel_id=1, source_target_pairs={{0,8},{4,12},{8,0},{12,4},{1,9},{5,13},{9,1},{13,5},{2,10},{6,14},... | collective-permute-start | bytes 2064392 | tf_op jit(solution)/shard_map/ppermute | solution.py:20
  13.7 28.9 %collective-permute-start.1 = (f32[7,3,32,256]{3,2,1,0:T(8,128)}, f32[7,3,32,256]{3,2,1,0:T(8,128)S(1)}, u32[]{:S(2)}, u32[]{:S(2)}) collective-permute-start(f32[7,3,32,256]{3,2,1,0:T(8,128)} %get-tuple-element.23), channel_id=1, source_target_pairs={{0,16},{16,0},{1,17},{17,1},{2,18},{18,2},{3,19},{19,3},{4,20},{20... | collective-permute-start | bytes 2064392 | tf_op jit(solution)/shard_map/ppermute | solution.py:30
  14.4 28.2 %copy-start.10 = (f32[7]{0:T(128)S(1)}, f32[7]{0:T(128)}, u32[]{:S(2)}) copy-start(f32[7]{0:T(128)} %constant.69.clone) | copy-start | bytes 88
  14.4 29.7 %copy-start.7 = (f32[6,4,32,256]{3,2,1,0:T(8,128)}, f32[6,4,32,256]{3,2,1,0:T(8,128)S(1)}, u32[]{:S(2)}) copy-start(f32[6,4,32,256]{3,2,1,0:T(8,128)S(1)} %broadcast_dynamic-update-slice_fusion) | copy-start | bytes 2359300
  28.7 15.4 %copy-start.3 = (f32[7,3,32,256]{3,2,1,0:T(8,128)}, f32[7,3,32,256]{3,2,1,0:T(8,128)S(1)}, u32[]{:S(2)}) copy-start(f32[7,3,32,256]{3,2,1,0:T(8,128)S(1)} %collective-permute-done.2) | copy-start | bytes 2064388
  42.6 3.5 %copy-start.1 = (f32[7,3,32,256]{3,2,1,0:T(8,128)}, f32[7,3,32,256]{3,2,1,0:T(8,128)S(1)}, u32[]{:S(2)}) copy-start(f32[7,3,32,256]{3,2,1,0:T(8,128)S(1)} %collective-permute-done.1) | copy-start | bytes 2064388
  47.9 5.6 %copy-start.5 = (f32[7,10,32,256]{3,2,1,0:T(8,128)S(1)}, f32[7,10,32,256]{3,2,1,0:T(8,128)}, u32[]{:S(2)}) copy-start(f32[7,10,32,256]{3,2,1,0:T(8,128)} %get-tuple-element.21) | copy-start | bytes 6881284
  50.5 9.2 %collective-permute-start.4 = (f32[7,10,32,3]{2,0,3,1:T(8,128)}, f32[7,10,32,3]{2,0,3,1:T(8,128)}, u32[]{:S(2)}, u32[]{:S(2)}) collective-permute-start(f32[7,10,32,3]{2,0,3,1:T(8,128)} %copy.7), channel_id=1, source_target_pairs={{4,0},{8,4},{12,8},{0,12},{5,1},{9,5},{13,9},{1,13},{6,2},{10,6},{... | collective-permute-start | bytes 80648 | tf_op jit(solution)/shard_map/ppermute | solution.py:32
  53.2 7.9 %collective-permute-start.3 = (f32[7,10,32,3]{2,0,3,1:T(8,128)}, f32[7,10,32,3]{2,0,3,1:T(8,128)}, u32[]{:S(2)}, u32[]{:S(2)}) collective-permute-start(f32[7,10,32,3]{2,0,3,1:T(8,128)} %copy.6), channel_id=1, source_target_pairs={{0,4},{4,8},{8,12},{12,0},{1,5},{5,9},{9,13},{13,1},{2,6},{6,10},{... | collective-permute-start | bytes 80648 | tf_op jit(solution)/shard_map/ppermute | solution.py:30
  65.0 1.1 copy-start.2
  65.1 1.3 copy-start.4
  68.3 14.1 %collective-permute-start.6 = (f32[7,10,3,262]{3,2,1,0:T(4,128)S(1)}, f32[7,10,3,262]{3,2,1,0:T(4,128)S(1)}, u32[]{:S(2)}, u32[]{:S(2)}) collective-permute-start(f32[7,10,3,262]{3,2,1,0:T(4,128)S(1)} %get-tuple-element.18), channel_id=1, source_target_pairs={{1,0},{2,1},{3,2},{0,3},{5,4},{6,5},{7,6},{4,7},{9,8},{10,9},{11,1... | collective-permute-start | bytes 660248 | tf_op jit(solution)/shard_map/ppermute | solution.py:32
  72.2 20.3 %collective-permute-start.5 = (f32[7,10,3,262]{3,2,1,0:T(4,128)S(1)}, f32[7,10,3,262]{3,2,1,0:T(4,128)S(1)}, u32[]{:S(2)}, u32[]{:S(2)}) collective-permute-start(f32[7,10,3,262]{3,2,1,0:T(4,128)S(1)} %get-tuple-element.17), channel_id=1, source_target_pairs={{0,1},{1,2},{2,3},{3,0},{4,5},{5,6},{6,7},{7,4},{8,9},{9,10},{10,1... | collective-permute-start | bytes 660248 | tf_op jit(solution)/shard_map/ppermute | solution.py:30
  99.4 5.0 %copy-start.6 = (f32[6,5,32,256]{3,2,1,0:T(8,128)S(1)}, f32[6,5,32,256]{3,2,1,0:T(8,128)}, u32[]{:S(2)}) copy-start(f32[6,5,32,256]{3,2,1,0:T(8,128)} %add_multiply_fusion.3) | copy-start | bytes 2949124
  99.4 5.0 %copy-start.8 = (f32[6,4,32,256]{3,2,1,0:T(8,128)S(1)}, f32[6,4,32,256]{3,2,1,0:T(8,128)}, u32[]{:S(2)}) copy-start(f32[6,4,32,256]{3,2,1,0:T(8,128)} %copy-done.7) | copy-start | bytes 2359300
  99.4 5.0 %copy-start.9 = (f32[6,4,32,256]{3,2,1,0:T(8,128)S(1)}, f32[6,4,32,256]{3,2,1,0:T(8,128)}, u32[]{:S(2)}) copy-start(f32[6,4,32,256]{3,2,1,0:T(8,128)} %param.5) | copy-start | bytes 2359300
  105.2 1.6 %copy-start.11 = (s32[4]{0:T(128)S(1)}, s32[4]{0:T(128)}, u32[]{:S(2)}) copy-start(s32[4]{0:T(128)} %param.8) | copy-start | bytes 52
Sparse Core Ops, SparseCore 0:
  106.9 31.6 all-reduce.1
where the time goes:
time: 149 us; the launch traced here: 148 us
  waiting for transfers between devices  73.5 us (49%)
  other arithmetic  36.1 us (24%)
  between operations  13.8 us (9%)
  local copies, waits for them, and re-layouts  11 us (7%)
  starting transfers between devices  9.39 us (6%)
  matrix products  4.34 us (3%)
    psum x1, waiting for transfers between devices, apply_filter(): coefficients = lax.psum(coefficients, 'theta')  31.6 us
    ppermute x3, waiting for transfers between devices, with_halo(): lax.ppermute(tail, axis, [(i, (i + 1) % count) for i in range(count)])  23.9 us
    ppermute x3, waiting for transfers between devices, with_halo(): lax.ppermute(head, axis, [((i + 1) % count, i) for i in range(count)])  18 us
    add x2, other arithmetic, face_fluxes(): return upwind_part + downwind_part  10.9 us
    concatenate x2, other arithmetic, with_halo(): jnp.concatenate([lax.ppermute(tail, axis, [(i, (i + 1) % count) for i in...  8.27 us
    ppermute x3, starting transfers between devices, with_halo(): lax.ppermute(head, axis, [((i + 1) % count, i) for i in range(count)])  7.17 us
    mul x1, other arithmetic, tendency(): weighted = face_radius * radial_flux  5.18 us
    slice x3, local copies, waits for them, and re-layouts, with_halo(): lax.slice_in_dim(cells, cells.shape[dim] - width, cells.shape[dim], axis=...  4.38 us
  transfers between devices with their start and end apart: 8, of which 5 were waited for; matrix products, arithmetic and copies ran while one was open for 11% of the time, Pallas kernels for 0%

commit v1 on v0

--- a/solution.py
+++ b/solution.py
@@ -1,3 +1,4 @@
+import functools
 import math
 import jax
 import jax.numpy as jnp
@@ -12,6 +13,13 @@
 liquid_ratio = 4.4
 gas_ratio = 1.4
 liquid_stiffness = 0.6
+
+
+def replace_the_racks(vector, ax_name):
+    return lax.all_gather(vector, ax_name).sum(axis=0)
+
+
+begin_copies_here = functools.partial(replace_the_racks, ax_name="theta")
 
 
 def passed_along(value, axis, steps):
@@ -155,7 +163,7 @@
     coefficients = jnp.einsum(
         "vizt,tk->vizk", cycle_block, fourier_table, precision=lax.Precision.HIGHEST
     )
-    coefficients = lax.psum(coefficients, "theta")
+    coefficients = begin_copies_here(coefficients)
     coefficients = coefficients * weights[None, :, None, :]
     return jnp.einsum("vizk,tk->vizt", coefficients, fourier_table, precision=lax.Precision.HIGHEST)
 

time: 149 us -> 136 us (0.913)
  waiting for transfers between devices: 73.5 us -> 60.4 us
  other arithmetic: 36.1 us -> 37.7 us
    psum x1 -> x0, waiting for transfers between devices: 31.6 us -> none  [apply_filter(): coefficients = lax.psum(coefficients, 'theta')]
    all_gather x0 -> x1, waiting for transfers between devices: none -> 18.5 us  [replace_the_racks(): return lax.all_gather(vector, ax_name).sum(axis=0)]
    reduce_sum x0 -> x1, other arithmetic: none -> 1.6 us  [replace_the_racks(): return lax.all_gather(vector, ax_name).sum(axis=0)]
  transfers between devices with their start and end apart: 8 -> 8, of which waited for: 5 -> 5; matrix products, arithmetic and copies ran while one was open for 11% -> 12% of each run, Pallas kernels for 0% -> 0%
where the time goes in v1:
time: 136 us
  waiting for transfers between devices  60.4 us (44%)
  other arithmetic  37.7 us (28%)
  between operations  13.8 us (10%)
  local copies, waits for them, and re-layouts  11 us (8%)
  starting transfers between devices  9.39 us (7%)
  matrix products  3.35 us (2%)
    ppermute x3, waiting for transfers between devices, with_halo(): lax.ppermute(tail, axis, [(i, (i + 1) % count) for i in range(count)])  23.9 us
    all_gather x1, waiting for transfers between devices, replace_the_racks(): return lax.all_gather(vector, ax_name).sum(axis=0)  18.5 us
    ppermute x3, waiting for transfers between devices, with_halo(): lax.ppermute(head, axis, [((i + 1) % count, i) for i in range(count)])  18 us
    add x2, other arithmetic, face_fluxes(): return upwind_part + downwind_part  10.9 us
    concatenate x2, other arithmetic, with_halo(): jnp.concatenate([lax.ppermute(tail, axis, [(i, (i + 1) % count) for i in...  8.27 us
    ppermute x3, starting transfers between devices, with_halo(): lax.ppermute(head, axis, [((i + 1) % count, i) for i in range(count)])  7.17 us
    mul x1, other arithmetic, tendency(): weighted = face_radius * radial_flux  5.18 us
    slice x3, local copies, waits for them, and re-layouts, with_halo(): lax.slice_in_dim(cells, cells.shape[dim] - width, cells.shape[dim], axis=...  4.38 us
  transfers between devices with their start and end apart: 8, of which 5 were waited for; matrix products, arithmetic and copies ran while one was open for 12% of the time, Pallas kernels for 0%

profile of v1, /device:TPU:0, one launch (start us, length us, event | category | flops | bytes accessed | tf_op | source)
XLA Modules:
  0.0 135.7 jit_solution(9670159649851151030)
XLA Ops:
  6.6 1.4 %bitcast_dynamic-update-slice_fusion = (f32[6,4,32,256]{3,2,1,0:T(8,128)S(1)}, f32[4,32,256]{2,1,0:T(8,128)S(1)}) fusion(f32[6,4,32,256]{3,2,1,0:T(8,128)S(1)} %broadcast_dynamic-update-slice_fusion.1, f32[6,4,32,256]{3,2,1,0:T(8,128)} %param.6, f32[4]{0:T(128)S(1)} %get-tuple-element.28, s32[4,32,256]{2,1,0:T(8,128)} %param.7), kind=kLoop, calls=%fused_computation.96 | loop fusion | flops 622592 | bytes 1049088
  7.9 0.1 copy-done
  8.0 1.2 fusion.11
  9.2 3.0 %collective-permute-start.2 = (f32[7,3,32,256]{3,2,1,0:T(8,128)}, f32[7,3,32,256]{3,2,1,0:T(8,128)S(1)}, u32[]{:S(2)}, u32[]{:S(2)}) collective-permute-start(f32[7,3,32,256]{3,2,1,0:T(8,128)} %get-tuple-element.24), channel_id=1, source_target_pairs={{16,0},{0,16},{17,1},{1,17},{18,2},{2,18},{19,3},{3,19},{20,4},{4,... | collective-permute-start | bytes 2064392 | tf_op jit(solution)/shard_map/ppermute | solution.py:40
  12.2 1.5 %collective-permute-start = (f32[7,3,32,256]{3,2,1,0:T(8,128)}, f32[7,3,32,256]{3,2,1,0:T(8,128)}, u32[]{:S(2)}, u32[]{:S(2)}) collective-permute-start(f32[7,3,32,256]{3,2,1,0:T(8,128)} %get-tuple-element.24), channel_id=1, source_target_pairs={{0,8},{4,12},{8,0},{12,4},{1,9},{5,13},{9,1},{13,5},{2,10},{6,14},... | collective-permute-start | bytes 2064392 | tf_op jit(solution)/shard_map/ppermute | solution.py:28
  13.7 0.5 collective-permute-start.1
  14.2 0.1 divide_dynamic-update-slice_fusion
  14.4 0.0 copy-start.10
  14.4 0.0 copy-start.7
  14.4 0.6 fusion.47
  15.0 13.7 %collective-permute-done.2 = f32[7,3,32,256]{3,2,1,0:T(8,128)S(1)} collective-permute-done((f32[7,3,32,256]{3,2,1,0:T(8,128)}, f32[7,3,32,256]{3,2,1,0:T(8,128)S(1)}, u32[]{:S(2)}, u32[]{:S(2)}) %collective-permute-start.2) | collective-permute-done | bytes 688160 | tf_op jit(solution)/shard_map/ppermute | solution.py:40
  28.7 0.1 broadcast_select_fusion
  28.8 13.8 %collective-permute-done.1 = f32[7,3,32,256]{3,2,1,0:T(8,128)S(1)} collective-permute-done((f32[7,3,32,256]{3,2,1,0:T(8,128)}, f32[7,3,32,256]{3,2,1,0:T(8,128)S(1)}, u32[]{:S(2)}, u32[]{:S(2)}) %collective-permute-start.1) | collective-permute-done | bytes 688160 | tf_op jit(solution)/shard_map/ppermute | solution.py:38
  42.6 1.5 %multiply_select_fusion = f32[7,3,32,256]{3,2,1,0:T(8,128)S(1)} fusion(f32[7,3,32,256]{3,2,1,0:T(8,128)S(1)} %collective-permute-done.1, f32[7,3,32,256]{3,2,1,0:T(8,128)} %collective-permute-done, f32[7]{0:T(128)S(1)} %copy-done.10, pred[]{:T(512)S(6)} %eq.25), kind=kLoop, calls=%fused_computation.37 | loop fusion | flops 344064 | bytes 2064413 | tf_op jit(solution)/shard_map/jit(_where)/select_n | solution.py:187
  44.2 1.9 %pad_maximum_fusion.2 = (f32[7,10,32,256]{3,2,1,0:T(8,128)}, f32[7,10,32,256]{3,2,1,0:T(8,128)S(1)}) fusion(f32[7,3,32,256]{3,2,1,0:T(8,128)S(1)} %broadcast_select_fusion, f32[1,4,32,256]{3,2,1,0:T(8,128)S(1)} %bitcast.50, f32[6,4,32,256]{3,2,1,0:T(8,128)S(1)} %copy-done, f32[7,3,32,256]{3,2,1,0:T(8,128)S(1)} %multiply_select_fusion, ...), kind=kLoop, calls=%fused_computation.2 | loop fusion | flops 2867200 | bytes 8257536 | tf_op jit(solution)/shard_map/concatenate | solution.py:189
  46.1 1.8 %fusion.56 = (f32[7,10,32,3]{3,2,1,0:T(8,128)}, f32[7,10,32,3]{3,2,1,0:T(8,128)}) fusion(f32[7,10,32,256]{3,2,1,0:T(8,128)S(1)} %get-tuple-element.22), kind=kLoop, calls=%fused_computation.127 | loop fusion | bytes 107520 | tf_op jit(solution)/shard_map/slice | solution.py:35
  47.9 2.6 %copy.7 = f32[7,10,32,3]{2,0,3,1:T(8,128)} copy(f32[7,10,32,3]{3,2,1,0:T(8,128)} %get-tuple-element.20) | data formatting | bytes 53760 | tf_op jit(solution)/shard_map/slice | solution.py:34
  50.5 0.3 collective-permute-start.4
  50.8 2.4 %copy.6 = f32[7,10,32,3]{2,0,3,1:T(8,128)} copy(f32[7,10,32,3]{3,2,1,0:T(8,128)} %get-tuple-element.19) | data formatting | bytes 53760 | tf_op jit(solution)/shard_map/slice | solution.py:35
  53.2 0.2 collective-permute-start.3
  53.4 0.1 multiply_dynamic-update-slice_fusion
  53.5 0.1 add_dynamic-update-slice_fusion
  53.7 0.1 fusion.16
  53.8 0.7 add_multiply_fusion
  54.5 5.2 %add_multiply_fusion.3 = f32[6,5,32,256]{3,2,1,0:T(8,128)} fusion(f32[6,10,32,256]{3,2,1,0:T(8,128)S(1)} %get-tuple-element.16, f32[6,10,32,256]{3,2,1,0:T(8,128)S(1)} %get-tuple-element.15, f32[5]{0:T(128)S(1)} %add_convert_fusion), kind=kLoop, calls=%fused_computation.20 | loop fusion | flops 31948800 | bytes 10813460 | tf_op jit(solution)/shard_map/mul | solution.py:122
  59.7 0.0 collective-permute-done.4
  59.7 1.4 %copy.9 = f32[7,10,32,3]{3,2,1,0:T(8,128)S(1)} copy(f32[7,10,32,3]{2,0,3,1:T(8,128)} %collective-permute-done.4) | data formatting | bytes 53760 | tf_op jit(solution)/shard_map/ppermute | solution.py:40
  61.1 1.4 %copy.8 = f32[7,10,32,3]{3,2,1,0:T(8,128)S(1)} copy(f32[7,10,32,3]{2,0,3,1:T(8,128)} %collective-permute-done.3) | data formatting | bytes 53760 | tf_op jit(solution)/shard_map/ppermute | solution.py:38
  62.5 2.6 %pad_maximum_fusion.1 = f32[7,10,32,262]{3,2,1,0:T(8,128)S(1)} fusion(f32[7,10,32,3]{3,2,1,0:T(8,128)S(1)} %copy.9, f32[7,3,32,256]{3,2,1,0:T(8,128)} %copy-done.3, f32[1,4,32,256]{3,2,1,0:T(8,128)S(1)} %bitcast.51, f32[6,4,32,256]{3,2,1,0:T(8,128)S(1)} %copy-done, f32[7,3,32,256]{3,2,1,0:T(8,128)} %copy-done.1, f32[7,10,32,3]{3,2,1,0:T(8,128)S(1)} %copy.8), kind=kLoop, calls=%fused_computation.1 | loop fusion | flops 2934400 | bytes 4695040 | tf_op jit(solution)/shard_map/concatenate | solution.py:36
  65.1 0.2 fusion.55
  65.2 0.9 copy-done.2
  66.2 0.2 copy-done.4
  66.4 0.2 multiply_dynamic-update-slice_fusion.1
  66.6 0.3 fusion.26
  66.8 0.3 fusion.25
  67.1 0.3 fusion.23
  67.4 0.3 fusion.22
  67.7 0.3 fusion.20
  68.0 0.3 add_multiply_fusion.1
  68.4 3.9 %collective-permute-start.6 = (f32[7,10,3,262]{3,2,1,0:T(4,128)S(1)}, f32[7,10,3,262]{3,2,1,0:T(4,128)S(1)}, u32[]{:S(2)}, u32[]{:S(2)}) collective-permute-start(f32[7,10,3,262]{3,2,1,0:T(4,128)S(1)} %get-tuple-element.18), channel_id=1, source_target_pairs={{1,0},{2,1},{3,2},{0,3},{5,4},{6,5},{7,6},{4,7},{9,8},{10,9},{11,1... | collective-permute-start | bytes 660248 | tf_op jit(solution)/shard_map/ppermute | solution.py:40
  72.2 0.0 collective-permute-start.5
  72.2 5.9 %divide_add_fusion = f32[6,4,32,257]{3,2,1,0:T(8,128)S(1)} fusion(f32[6,4,32,262]{3,2,1,0:T(8,128)S(1)} %get-tuple-element.14, f32[6,4,32,262]{3,2,1,0:T(8,128)S(1)} %get-tuple-element.13), kind=kLoop, calls=%fused_computation.13 | loop fusion | flops 25461504 | bytes 8684544 | tf_op jit(solution)/shard_map/add | solution.py:111
  78.1 4.3 %collective-permute-done.6 = f32[7,10,3,262]{3,2,1,0:T(4,128)S(1)} collective-permute-done((f32[7,10,3,262]{3,2,1,0:T(4,128)S(1)}, f32[7,10,3,262]{3,2,1,0:T(4,128)S(1)}, u32[]{:S(2)}, u32[]{:S(2)}) %collective-permute-start.6) | collective-permute-done | bytes 220112 | tf_op jit(solution)/shard_map/ppermute | solution.py:40
  82.4 10.1 %collective-permute-done.5 = f32[7,10,3,262]{3,2,1,0:T(4,128)S(1)} collective-permute-done((f32[7,10,3,262]{3,2,1,0:T(4,128)S(1)}, f32[7,10,3,262]{3,2,1,0:T(4,128)S(1)}, u32[]{:S(2)}, u32[]{:S(2)}) %collective-permute-start.5) | collective-permute-done | bytes 220112 | tf_op jit(solution)/shard_map/ppermute | solution.py:38
  92.5 5.7 %pad_maximum_fusion = f32[7,10,38,262]{3,2,1,0:T(8,128)S(1)} fusion(f32[7,10,3,262]{3,2,1,0:T(4,128)S(1)} %collective-permute-done.6, f32[7,10,32,3]{3,2,1,0:T(8,128)S(1)} %copy.9, f32[7,3,32,256]{3,2,1,0:T(8,128)S(1)} %copy-done.4, f32[1,4,32,256]{3,2,1,0:T(8,128)S(1)} %bitcast.58, f32[6,4,32,256]{3,2,1,0:T(8,128)S(1)} %copy-done, ...), kind=kLoop, calls=%fused_computation | loop fusion | flops 4878440 | bytes 5575360 | tf_op jit(solution)/shard_map/concatenate | solution.py:36
  98.2 0.2 multiply_dynamic-update-slice_fusion.2
  98.4 0.1 fusion.32
  98.5 0.1 fusion.31
  98.6 0.2 add_dynamic-update-slice_fusion.1
  98.8 0.2 fusion.30
  98.9 0.1 fusion.28
  99.1 0.3 add_multiply_fusion.2
  99.4 0.0 copy-start.8
  99.4 0.0 copy-start.9
  99.4 5.0 %divide_add_fusion.1 = f32[6,4,33,256]{3,2,1,0:T(8,128)S(1)} fusion(f32[6,4,38,256]{3,2,1,0:T(8,128)S(1)} %get-tuple-element.12, f32[6,4,38,256]{3,2,1,0:T(8,128)S(1)} %get-tuple-element.11), kind=kLoop, calls=%fused_computation.17 | loop fusion | flops 26155008 | bytes 8921088 | tf_op jit(solution)/shard_map/add | solution.py:111
  104.5 0.7 fusion.7
  105.2 0.0 copy-start.11
  105.2 1.6 %fusion.48 = f32[6,4,32,128]{3,2,1,0:T(8,128)} fusion(f32[6,4,32,256]{3,2,1,0:T(8,128)S(1)} %fusion.7, f32[256,64]{1,0:T(8,128)S(1)} %get-tuple-element.26, f32[256,64]{1,0:T(8,128)S(1)} %get-tuple-element.25), kind=kOutput, calls=%fused_computation.112 | convolution fusion | flops 302022656 | bytes 1310720 | tf_op jit(solution)/shard_map/vizt,tk->vizk/dot_general | solution.py:163
  106.8 0.0 all-gather.3.cloned.1.call-update
  106.9 0.1 fusion.49
  106.9 0.1 pad_maximum_fusion.8
  107.0 18.5 %all-gather.3.cloned.1.call-done = f32[24,4,32,128]{3,2,1,0:T(8,128)} async-done(((f32[6,4,32,128]{3,2,1,0:T(8,128)}), f32[24,4,32,128]{3,2,1,0:T(8,128)}) %all-gather.3.cloned.1.call-update) | async-done | bytes 1572880 | tf_op jit(solution)/shard_map/all_gather | solution.py:19
  125.5 1.6 %reduce_sum.9 = f32[6,4,32,128]{3,2,1,0:T(8,128)S(1)} reduce(f32[4,6,4,32,128]{4,3,2,1,0:T(8,128)} %bitcast.59, f32[]{:T(128)} %constant.39.clone.1), dimensions={0}, to_apply=%region_0.1 | reduce | flops 294912 | bytes 1966084 | tf_op jit(solution)/shard_map/reduce_sum | solution.py:19
  127.1 1.7 %convolution_select_fusion = f32[6,4,32,256]{3,2,1,0:T(8,128)} fusion(f32[6,4,32,256]{3,2,1,0:T(8,128)S(1)} %fusion.7, f32[6,4,32,128]{3,2,1,0:T(8,128)S(1)} %reduce_sum.9, pred[]{:T(512)S(6)} %eq.25, f32[4,128]{1,0:T(4,128)S(1)} %pad_maximum_fusion.8, f32[256,64]{1,0:T(8,128)S(1)} %get-tuple-element.26, f32[256,64]{1,0:T(8,128)S(1)} %get-tuple-element.25), kind=kOutput, calls=%fused_computation.9 | convolution fusion | flops 302317568 | bytes 2099201 | tf_op jit(solution)/shard_map/vizk,tk->vizt/dot_general | solution.py:168
  (31 shorter events, 0.3 us)
Async XLA Ops:
  6.5 1.5 %copy-start = (f32[6,4,32,256]{3,2,1,0:T(8,128)S(1)}, f32[6,4,32,256]{3,2,1,0:T(8,128)}, u32[]{:S(2)}) copy-start(f32[6,4,32,256]{3,2,1,0:T(8,128)} %param.6) | copy-start | bytes 2359300
  6.5 118.9 %all-gather.3.cloned.1.call-start = ((), (), s32[]{:S(2)}) async-start(), calls=%async_computation | async-start | bytes 1966080 | tf_op jit(solution)/shard_map/all_gather | solution.py:19
  9.2 19.5 %collective-permute-start.2 = (f32[7,3,32,256]{3,2,1,0:T(8,128)}, f32[7,3,32,256]{3,2,1,0:T(8,128)S(1)}, u32[]{:S(2)}, u32[]{:S(2)}) collective-permute-start(f32[7,3,32,256]{3,2,1,0:T(8,128)} %get-tuple-element.24), channel_id=1, source_target_pairs={{16,0},{0,16},{17,1},{1,17},{18,2},{2,18},{19,3},{3,19},{20,4},{4,... | collective-permute-start | bytes 2064392 | tf_op jit(solution)/shard_map/ppermute | solution.py:40
  12.2 30.4 %collective-permute-start = (f32[7,3,32,256]{3,2,1,0:T(8,128)}, f32[7,3,32,256]{3,2,1,0:T(8,128)}, u32[]{:S(2)}, u32[]{:S(2)}) collective-permute-start(f32[7,3,32,256]{3,2,1,0:T(8,128)} %get-tuple-element.24), channel_id=1, source_target_pairs={{0,8},{4,12},{8,0},{12,4},{1,9},{5,13},{9,1},{13,5},{2,10},{6,14},... | collective-permute-start | bytes 2064392 | tf_op jit(solution)/shard_map/ppermute | solution.py:28
  13.7 28.9 %collective-permute-start.1 = (f32[7,3,32,256]{3,2,1,0:T(8,128)}, f32[7,3,32,256]{3,2,1,0:T(8,128)S(1)}, u32[]{:S(2)}, u32[]{:S(2)}) collective-permute-start(f32[7,3,32,256]{3,2,1,0:T(8,128)} %get-tuple-element.23), channel_id=1, source_target_pairs={{0,16},{16,0},{1,17},{17,1},{2,18},{18,2},{3,19},{19,3},{4,20},{20... | collective-permute-start | bytes 2064392 | tf_op jit(solution)/shard_map/ppermute | solution.py:38
  14.4 28.3 %copy-start.10 = (f32[7]{0:T(128)S(1)}, f32[7]{0:T(128)}, u32[]{:S(2)}) copy-start(f32[7]{0:T(128)} %constant.69.clone) | copy-start | bytes 88
  14.4 29.7 %copy-start.7 = (f32[6,4,32,256]{3,2,1,0:T(8,128)}, f32[6,4,32,256]{3,2,1,0:T(8,128)S(1)}, u32[]{:S(2)}) copy-start(f32[6,4,32,256]{3,2,1,0:T(8,128)S(1)} %broadcast_dynamic-update-slice_fusion) | copy-start | bytes 2359300
  28.7 15.4 %copy-start.3 = (f32[7,3,32,256]{3,2,1,0:T(8,128)}, f32[7,3,32,256]{3,2,1,0:T(8,128)S(1)}, u32[]{:S(2)}) copy-start(f32[7,3,32,256]{3,2,1,0:T(8,128)S(1)} %collective-permute-done.2) | copy-start | bytes 2064388
  42.6 3.5 %copy-start.1 = (f32[7,3,32,256]{3,2,1,0:T(8,128)}, f32[7,3,32,256]{3,2,1,0:T(8,128)S(1)}, u32[]{:S(2)}) copy-start(f32[7,3,32,256]{3,2,1,0:T(8,128)S(1)} %collective-permute-done.1) | copy-start | bytes 2064388
  47.9 5.6 %copy-start.5 = (f32[7,10,32,256]{3,2,1,0:T(8,128)S(1)}, f32[7,10,32,256]{3,2,1,0:T(8,128)}, u32[]{:S(2)}) copy-start(f32[7,10,32,256]{3,2,1,0:T(8,128)} %get-tuple-element.21) | copy-start | bytes 6881284
  50.5 9.2 %collective-permute-start.4 = (f32[7,10,32,3]{2,0,3,1:T(8,128)}, f32[7,10,32,3]{2,0,3,1:T(8,128)}, u32[]{:S(2)}, u32[]{:S(2)}) collective-permute-start(f32[7,10,32,3]{2,0,3,1:T(8,128)} %copy.7), channel_id=1, source_target_pairs={{4,0},{8,4},{12,8},{0,12},{5,1},{9,5},{13,9},{1,13},{6,2},{10,6},{... | collective-permute-start | bytes 80648 | tf_op jit(solution)/shard_map/ppermute | solution.py:40
  53.2 7.9 %collective-permute-start.3 = (f32[7,10,32,3]{2,0,3,1:T(8,128)}, f32[7,10,32,3]{2,0,3,1:T(8,128)}, u32[]{:S(2)}, u32[]{:S(2)}) collective-permute-start(f32[7,10,32,3]{2,0,3,1:T(8,128)} %copy.6), channel_id=1, source_target_pairs={{0,4},{4,8},{8,12},{12,0},{1,5},{5,9},{9,13},{13,1},{2,6},{6,10},{... | collective-permute-start | bytes 80648 | tf_op jit(solution)/shard_map/ppermute | solution.py:38
  65.1 1.1 copy-start.2
  65.1 1.3 copy-start.4
  68.4 14.1 %collective-permute-start.6 = (f32[7,10,3,262]{3,2,1,0:T(4,128)S(1)}, f32[7,10,3,262]{3,2,1,0:T(4,128)S(1)}, u32[]{:S(2)}, u32[]{:S(2)}) collective-permute-start(f32[7,10,3,262]{3,2,1,0:T(4,128)S(1)} %get-tuple-element.18), channel_id=1, source_target_pairs={{1,0},{2,1},{3,2},{0,3},{5,4},{6,5},{7,6},{4,7},{9,8},{10,9},{11,1... | collective-permute-start | bytes 660248 | tf_op jit(solution)/shard_map/ppermute | solution.py:40
  72.2 20.3 %collective-permute-start.5 = (f32[7,10,3,262]{3,2,1,0:T(4,128)S(1)}, f32[7,10,3,262]{3,2,1,0:T(4,128)S(1)}, u32[]{:S(2)}, u32[]{:S(2)}) collective-permute-start(f32[7,10,3,262]{3,2,1,0:T(4,128)S(1)} %get-tuple-element.17), channel_id=1, source_target_pairs={{0,1},{1,2},{2,3},{3,0},{4,5},{5,6},{6,7},{7,4},{8,9},{9,10},{10,1... | collective-permute-start | bytes 660248 | tf_op jit(solution)/shard_map/ppermute | solution.py:38
  99.4 5.0 %copy-start.6 = (f32[6,5,32,256]{3,2,1,0:T(8,128)S(1)}, f32[6,5,32,256]{3,2,1,0:T(8,128)}, u32[]{:S(2)}) copy-start(f32[6,5,32,256]{3,2,1,0:T(8,128)} %add_multiply_fusion.3) | copy-start | bytes 2949124
  99.4 5.0 %copy-start.8 = (f32[6,4,32,256]{3,2,1,0:T(8,128)S(1)}, f32[6,4,32,256]{3,2,1,0:T(8,128)}, u32[]{:S(2)}) copy-start(f32[6,4,32,256]{3,2,1,0:T(8,128)} %copy-done.7) | copy-start | bytes 2359300
  99.4 5.0 %copy-start.9 = (f32[6,4,32,256]{3,2,1,0:T(8,128)S(1)}, f32[6,4,32,256]{3,2,1,0:T(8,128)}, u32[]{:S(2)}) copy-start(f32[6,4,32,256]{3,2,1,0:T(8,128)} %param.5) | copy-start | bytes 2359300
  105.2 1.7 %copy-start.11 = (s32[4]{0:T(128)S(1)}, s32[4]{0:T(128)}, u32[]{:S(2)}) copy-start(s32[4]{0:T(128)} %param.8) | copy-start | bytes 52
Sparse Core Ops, SparseCore 0:
  107.0 18.4 all-gather.2
